TPU v7x, 128 devices: a whole 4x4x4 slice. The times are simulated.
128 devices in a mesh: grid: 16 (over y, z_lo, core), dom: 8 (over x, z_hi).
Axes of the slice: x: 4, y: 4, z: 4 (z_hi: 2, z_lo: 2; z = z_hi * 2 + z_lo), core: 2. Of those that a mesh axis runs over, the one named last changes fastest.
Arguments:
- values: float32 [16, 32, 4, 4, 8, 8, 128], P('grid', 'dom'), may hold values from -2 to 2
- levels: int32 [16, 6], P('grid'), may hold values from 0 to 7, as said below
- coefficients: int32 [16], P('grid'), may hold values from -3 to 3, as said below
Outputs:
- combined: float32 [16, 32, 4, 4, 8, 8, 128], P('grid', 'dom')
Inputs may be any that keep to these rules, and one draw needn't show every extreme that they name: levels[g, k] is grid g's level along dimension k + 1. With L_k the base-two logarithm of that dimension's extent (32, 4, 4, 8, 8, 128), each entry lies between L_k - 2 and L_k, and the shortfalls L_k - levels[g, k] of one grid add up to 2 at most. `coefficients`: every coefficient is nonzero.
All inputs are finite; a program needn't handle non-finite values.
Results may differ from a plain program's by a relative error of at most 0.0003.
Values sent between devices are 32-bit elements; how exact they have to be, the bound alone decides.
No kernel may reach another device: no remote copies, remote signals or barrier semaphores. Data moves between devices by JAX's collectives and lax.ppermute only.
A program may use at most 64 MiB of HBM per device.

v0:
```python
import jax
import jax.numpy as jnp
import numpy as np
from jax import lax
from jax.sharding import PartitionSpec as P

PRECISE = lax.Precision.HIGHEST


def cut_along(x, dim, peers):
    before, after = (x.shape[:dim], x.shape[dim + 1 :])
    return jnp.moveaxis(x.reshape(*before, peers, -1, *after), dim, 0)


def sent_and_summed(x, axis, dim):
    parts = cut_along(x, dim, lax.axis_size(axis))
    arrived = lax.all_to_all(parts, axis, split_axis=0, concat_axis=0, tiled=True)
    return arrived.sum(axis=0)


def laid_out(parts, dim):
    parts = jnp.moveaxis(parts, 0, dim)
    shape = parts.shape
    return parts.reshape(*shape[:dim], shape[dim] * shape[dim + 1], *shape[dim + 2 :])


def from_everyone(x, axis):
    copies = jnp.broadcast_to(x, (lax.axis_size(axis), *x.shape))
    return lax.all_to_all(copies, axis, split_axis=0, concat_axis=0, tiled=True)


def collect(x, axis, dim):
    return laid_out(from_everyone(x, axis), dim)


def coarse_position(numerator, level_now):
    while numerator > 0 and numerator % 2 == 0:
        numerator = numerator // 2
        level_now = level_now - 1
    if numerator == 0:
        return 0
    return (1 << level_now - 1) + (numerator - 1) // 2


def parent_positions(position):
    level_now = position.bit_length()
    span_size = 1 << level_now - 1
    offset = position - span_size
    return [
        coarse_position(offset % span_size, level_now - 1),
        coarse_position((offset + 1) % span_size, level_now - 1),
    ]


def hier_table(points):
    matrix = np.eye(points)
    for position in range(1, points):
        for parent in parent_positions(position):
            matrix[position, parent] -= 0.5
    return matrix


def dehier_table(points):
    matrix = np.zeros((points, points))
    matrix[0, 0] = 1.0
    for position in range(1, points):
        row_now = np.zeros(points)
        row_now[position] = 1.0
        for parent in parent_positions(position):
            row_now = row_now + 0.5 * matrix[parent]
        matrix[position] = row_now
    return matrix


def nodal_order(points):
    placed = np.zeros(points, dtype=np.int64)
    for position in range(1, points):
        level_now = position.bit_length()
        offset = position - (1 << level_now - 1)
        placed[position] = (2 * offset + 1) * points // (1 << level_now)
    return placed


def nodal_table(matrix):
    placed = nodal_order(matrix.shape[0])
    result = np.zeros(matrix.shape)
    result[placed[:, None], placed[None, :]] = matrix
    return result


def local_hier(points):
    matrix = np.zeros((points, points + 1))
    matrix[0, 0] = 1.0
    for point in range(1, points):
        stride = point & -point
        matrix[point, point] = 1.0
        matrix[point, point - stride] -= 0.5
        matrix[point, point + stride] -= 0.5
    return matrix


def local_dehier(points):
    matrix = np.zeros((points + 1, points + 1))
    matrix[0, 0] = 1.0
    matrix[points, points] = 1.0
    stride = points // 2
    while stride >= 1:
        for point in range(stride, points, 2 * stride):
            row_now = np.zeros(points + 1)
            row_now[point] = 1.0
            matrix[point] = row_now + 0.5 * (matrix[point - stride] + matrix[point + stride])
        stride = stride // 2
    return matrix[:points]


def apply_table(grid_data, matrix, dim_index):
    letters = "abcdefg"[: grid_data.ndim]
    outputs = letters[:dim_index] + "z" + letters[dim_index + 1 :]
    formula = letters + ",z" + letters[dim_index] + "->" + outputs
    return jnp.einsum(formula, grid_data, jnp.asarray(matrix, dtype=jnp.float32), precision=PRECISE)


def tail_column(column, rank_count):
    return jnp.asarray(column, dtype=jnp.float32).reshape((-1,) + (1,) * (rank_count - 1))


def holding_mask(level_row, extents):
    holding = jnp.ones(extents, dtype=jnp.float32)
    for dim_index, points in enumerate(extents):
        limit = jnp.left_shift(jnp.int32(1), level_row[dim_index])
        inside = (jnp.arange(points, dtype=jnp.int32) < limit).astype(jnp.float32)
        shape_now = [1] * len(extents)
        shape_now[dim_index] = points
        holding = holding * inside.reshape(shape_now)
    return holding


def split_rows_mask(level_count, local_rows, rank_count):
    members = lax.axis_size("dom")
    total_rows = local_rows * members
    rows_here = lax.axis_index("dom") * local_rows + jnp.arange(local_rows, dtype=jnp.int32)
    spacing = jnp.right_shift(jnp.int32(total_rows), level_count)
    inside = (jnp.remainder(rows_here, spacing) == 0).astype(jnp.float32)
    return inside.reshape((local_rows,) + (1,) * (rank_count - 1))


def split_hierarchize(grid_data):
    members = lax.axis_size("dom")
    own_index = lax.axis_index("dom")
    first_row = grid_data[0]
    all_firsts = lax.all_gather(first_row[None], "dom", axis=0, tiled=True)
    coarse = apply_table(all_firsts, nodal_table(hier_table(members)), 0)
    new_first = lax.dynamic_index_in_dim(coarse, own_index, 0, keepdims=False)
    following = lax.dynamic_index_in_dim(all_firsts, (own_index + 1) % members, 0, keepdims=False)
    local_rows = grid_data.shape[0]
    matrix = local_hier(local_rows)
    result = (
        apply_table(grid_data, matrix[:, :local_rows], 0)
        + tail_column(matrix[:, local_rows], grid_data.ndim) * following[None]
    )
    return result.at[0].set(new_first)


def split_dehierarchize(grid_data):
    members = lax.axis_size("dom")
    own_index = lax.axis_index("dom")
    first_row = grid_data[0]
    all_firsts = lax.all_gather(first_row[None], "dom", axis=0, tiled=True)
    coarse = apply_table(all_firsts, nodal_table(dehier_table(members)), 0)
    new_first = lax.dynamic_index_in_dim(coarse, own_index, 0, keepdims=False)
    following = lax.dynamic_index_in_dim(coarse, (own_index + 1) % members, 0, keepdims=False)
    local_rows = grid_data.shape[0]
    grid_data = grid_data.at[0].set(new_first)
    matrix = local_dehier(local_rows)
    return (
        apply_table(grid_data, matrix[:, :local_rows], 0)
        + tail_column(matrix[:, local_rows], grid_data.ndim) * following[None]
    )


def body(values, levels, coefficients):
    grid_data = values[0]
    level_row = levels[0]
    weight = coefficients[0].astype(jnp.float32)
    extents = tuple(grid_data.shape[1:])
    local_rows = grid_data.shape[0]
    for dim_index in range(1, 6):
        grid_data = apply_table(grid_data, hier_table(grid_data.shape[dim_index]), dim_index)
    grid_data = split_hierarchize(grid_data)
    holding = (
        split_rows_mask(level_row[0], local_rows, grid_data.ndim)
        * holding_mask(level_row[1:], extents)[None]
    )
    weighted = weight * holding * grid_data
    merged = weighted.reshape((local_rows, extents[0] * extents[1]) + extents[2:])
    own_share = sent_and_summed(merged, "grid", 1)
    for dim_index in range(2, 5):
        own_share = apply_table(own_share, dehier_table(own_share.shape[dim_index]), dim_index)
    own_share = split_dehierarchize(own_share)
    gathered = collect(own_share, "grid", 1)
    combined = gathered.reshape(grid_data.shape)
    for dim_index in range(1, 3):
        combined = apply_table(combined, dehier_table(extents[dim_index - 1]), dim_index)
    return (holding * combined)[None]


def solution(mesh):
    in_specs = (P("grid", "dom", None, None, None, None, None), P("grid", None), P("grid"))
    out_specs = P("grid", "dom", None, None, None, None, None)
    return jax.shard_map(body, mesh=mesh, in_specs=in_specs, out_specs=out_specs, check_vma=False)
```

profile of v0, /device:TPU:1, one launch (start us, length us, event | category | flops | bytes accessed | tf_op | source)
XLA Modules:
  0.0 251.5 jit_solution(10346107945402557805)
XLA Ops:
  6.5 1.6 copy-done
  8.1 5.0 %fusion.20 = f32[4,4,4,8,8,128]{5,1,4,3,2,0:T(4,128)S(1)} fusion(f32[4,4,1,1,1,1]{1,0,5,4,3,2:T(4,128)} %constant.147, f32[4,4,4,8,8,128]{5,4,3,2,1,0:T(8,128)S(1)} %bitcast.96), kind=kOutput, calls=%fused_computation.24 | convolution fusion | flops 25165824 | bytes 4194368 | tf_op jit(solution)/shard_map/abcdef,zb->azcdef/dot_general | solution.py:120
  13.2 4.5 %fusion.23 = f32[4,4,4,8,8,128]{5,2,4,3,1,0:T(4,128)S(1)} fusion(f32[4,4,1,1,1,1]{1,0,5,4,3,2:T(4,128)S(1)} %copy-done.9, f32[4,4,4,8,8,128]{5,1,4,3,2,0:T(4,128)S(1)} %fusion.20), kind=kOutput, calls=%fused_computation.25 | convolution fusion | flops 25165824 | bytes 4194368 | tf_op jit(solution)/shard_map/abcdef,zc->abzdef/dot_general | solution.py:120
  17.7 3.0 %fusion.26 = f32[4,4,4,8,8,128]{5,3,4,2,1,0:T(8,128)S(1)} fusion(f32[8,8,1,1,1,1]{1,0,5,4,3,2:T(8,128)S(1)} %copy-done.7, f32[4,4,4,8,8,128]{5,2,4,3,1,0:T(4,128)S(1)} %fusion.23), kind=kOutput, calls=%fused_computation.26 | convolution fusion | flops 50331648 | bytes 4194560 | tf_op jit(solution)/shard_map/abcdef,zd->abczef/dot_general | solution.py:120
  20.8 2.1 fusion.12
  22.9 1.9 fusion.6
  24.8 1.3 copy-done.1
  26.1 0.8 slice.114
  27.7 0.7 fusion.39
  32.3 0.2 multiply_multiply_fusion.2
  32.5 68.7 %all-gather.3.cloned.1.call-done = f32[8,4,4,8,8,128]{5,4,3,2,1,0:T(8,128)} async-done(((f32[1,4,4,8,8,128]{5,4,3,2,1,0:T(8,128)}), f32[8,4,4,8,8,128]{5,4,3,2,1,0:T(8,128)}) %all-gather.3.cloned.1.call-update) | async-done | bytes 4194320 | tf_op jit(solution)/shard_map/all_gather | solution.py:151
  101.2 8.1 %fusion = f32[4,4,8,8,128,8]{4,5,3,2,1,0:T(8,128)S(1)} fusion(f32[8,8,1,1,1,1]{1,0,5,4,3,2:T(8,128)S(1)} %copy-done.11, f32[8,4,4,8,8,128]{5,4,3,2,1,0:T(8,128)} %all-gather.3.cloned.1.call-done), kind=kOutput, calls=%fused_computation | convolution fusion | flops 100663296 | bytes 8388864 | tf_op jit(solution)/shard_map/abcdef,za->zbcdef/dot_general | solution.py:120
  109.4 0.6 dynamic-slice_bitcast_fusion
  110.0 1.1 dynamic-slice_bitcast_fusion.1
  111.1 5.7 %multiply_add_fusion = f32[4,4,4,8,8,128]{5,0,4,3,2,1:T(4,128)} fusion(f32[4,4,1,1,1,1]{1,0,5,4,3,2:T(4,128)S(1)} %copy-done.13, f32[4,4,4,8,8,128]{5,4,3,2,1,0:T(8,128)S(1)} %copy-done.2, f32[4,4,8,8,128]{4,3,2,1,0:T(8,128)S(1)} %dynamic-slice_bitcast_fusion.1, f32[4]{0:T(128)S(1)} %copy-done.15), kind=kOutput, calls=%fused_computation.23 | convolution fusion | flops 26214400 | bytes 4718672 | tf_op jit(solution)/shard_map/abcdef,za->zbcdef/dot_general | solution.py:120
  116.8 13.8 %scatter.6 = f32[4,4,4,8,8,128]{5,0,4,3,2,1:T(4,128)} dynamic-update-slice(f32[4,4,4,8,8,128]{5,0,4,3,2,1:T(4,128)} %multiply_add_fusion, f32[1,4,4,8,8,128]{5,0,4,3,2,1:T(1,128)S(1)} %dynamic-slice_bitcast_fusion, s32[]{:T(128)} %constant.123.clone.1, s32[]{:T(128)} %constant.123.clone.1, s32[]{:T(128)} %constant.123.clone.1, s32[]{:T(128)} %constant.123.clone.1, s32[]{:T(128)} %constant.123.clone.1, ...) | dynamic-update-slice | bytes 1048580 | tf_op jit(solution)/shard_map/scatter | solution.py:161
  130.6 2.3 fusion.2
  133.0 32.1 %all_to_all.10 = f32[16,4,1,8,8,128]{5,1,4,3,2,0:T(4,128)S(1)} all-to-all(f32[16,4,1,8,8,128]{5,1,4,3,2,0:T(4,128)S(1)} %bitcast.97), channel_id=1, replica_groups=mesh['grid'=16,'dom'=8] {'grid'}, dimensions={0} | all-to-all | bytes 4194304 | tf_op jit(solution)/shard_map/all_to_all | solution.py:17
  165.1 0.3 bitcast_reduce_fusion
  165.4 0.3 copy-done.6
  165.8 0.3 convolution_bitcast_fusion.1
  166.1 0.3 convolution_bitcast_fusion
  166.4 0.3 fusion.40
  166.7 28.1 %all-gather = f32[8,8,8,128]{3,2,1,0:T(8,128)S(1)} all-gather(f32[1,8,8,128]{3,2,1,0:T(8,128)S(1)} %slice.115), channel_id=2, replica_groups=mesh['grid'=16,'dom'=8] {'dom'}, dimensions={0}, use_global_device_ids=true | all-gather | bytes 294912 | tf_op jit(solution)/shard_map/all_gather | solution.py:168
  194.8 0.5 fusion.34
  195.4 0.4 convolution_add_fusion
  195.9 0.2 broadcast_in_dim.4
  196.1 36.6 %all_to_all.11 = f32[16,4,1,8,8,128]{5,4,3,1,2,0:T(8,128)S(1)} all-to-all(f32[16,4,1,8,8,128]{5,4,3,1,2,0:T(8,128)S(1)} %broadcast_in_dim.4), channel_id=1, replica_groups=mesh['grid'=16,'dom'=8] {'grid'}, dimensions={0} | all-to-all | bytes 4194304 | tf_op jit(solution)/shard_map/all_to_all | solution.py:29
  232.7 4.3 %fusion.31 = f32[4,4,4,8,8,128]{5,1,4,3,2,0:T(4,128)S(1)} fusion(f32[4,4,1,1,1,1]{1,0,5,4,3,2:T(4,128)S(1)} %copy-done.8, f32[4,4,4,8,8,128]{5,4,3,0,2,1:T(8,128)S(1)} %bitcast.98), kind=kOutput, calls=%fused_computation.27 | convolution fusion | flops 25165824 | bytes 4194368 | tf_op jit(solution)/shard_map/abcdef,zb->azcdef/dot_general | solution.py:120
  237.0 4.3 %fusion.8 = f32[4,4,8,8,128,4]{4,5,3,2,1,0:T(4,128)S(1)} fusion(f32[4,4,1,1,1,1]{1,0,5,4,3,2:T(4,128)S(1)} %copy-done.8, f32[4,4,4,8,8,128]{5,1,4,3,2,0:T(4,128)S(1)} %fusion.31), kind=kOutput, calls=%fused_computation.11 | convolution fusion | flops 25165824 | bytes 4194368 | tf_op jit(solution)/shard_map/abcdef,zc->abzdef/dot_general | solution.py:120
  241.4 1.6 fusion.3
  243.0 1.6 copy.89
  (39 shorter events, 0.3 us)
Async XLA Ops:
  6.5 1.6 copy-start
  6.5 94.7 %all-gather.3.cloned.1.call-start = ((), (), s32[]{:S(2)}) async-start(), calls=%async_computation.2 | async-start | bytes 4718592 | tf_op jit(solution)/shard_map/all_gather | solution.py:151
  8.1 5.0 %copy-start.9 = (f32[4,4,1,1,1,1]{1,0,5,4,3,2:T(4,128)S(1)}, f32[4,4,1,1,1,1]{1,0,5,4,3,2:T(4,128)}, u32[]{:S(2)}) copy-start(f32[4,4,1,1,1,1]{1,0,5,4,3,2:T(4,128)} %constant.147) | copy-start | bytes 196
  13.2 4.5 %copy-start.7 = (f32[8,8,1,1,1,1]{1,0,5,4,3,2:T(8,128)S(1)}, f32[8,8,1,1,1,1]{1,0,5,4,3,2:T(8,128)}, u32[]{:S(2)}) copy-start(f32[8,8,1,1,1,1]{1,0,5,4,3,2:T(8,128)} %constant.148) | copy-start | bytes 772
  20.7 2.1 copy-start.3
  22.9 4.8 %copy-start.5 = (s32[1,6]{1,0:T(1,128)S(1)}, s32[1,6]{1,0:T(1,128)}, u32[]{:S(2)}) copy-start(s32[1,6]{1,0:T(1,128)} %param.24) | copy-start | bytes 76
  24.8 1.3 copy-start.1
  26.1 75.1 %copy-start.11 = (f32[8,8,1,1,1,1]{1,0,5,4,3,2:T(8,128)S(1)}, f32[8,8,1,1,1,1]{1,0,5,4,3,2:T(8,128)}, u32[]{:S(2)}) copy-start(f32[8,8,1,1,1,1]{1,0,5,4,3,2:T(8,128)} %constant.150) | copy-start | bytes 772
  101.2 9.9 %copy-start.13 = (f32[4,4,1,1,1,1]{1,0,5,4,3,2:T(4,128)S(1)}, f32[4,4,1,1,1,1]{1,0,5,4,3,2:T(4,128)}, u32[]{:S(2)}) copy-start(f32[4,4,1,1,1,1]{1,0,5,4,3,2:T(4,128)} %constant.146) | copy-start | bytes 196
  109.4 1.7 copy-start.2
  109.4 1.7 copy-start.15
  165.1 0.7 copy-start.6
  165.1 1.3 copy-start.4
  165.1 29.7 %copy-start.10 = (f32[8,8,1,1]{1,0,3,2:T(8,128)S(1)}, f32[8,8,1,1]{1,0,3,2:T(8,128)}, u32[]{:S(2)}) copy-start(f32[8,8,1,1]{1,0,3,2:T(8,128)} %constant.152) | copy-start | bytes 772
  165.1 30.3 %copy-start.12 = (f32[4,4,1,1]{1,0,3,2:T(4,128)S(1)}, f32[4,4,1,1]{1,0,3,2:T(4,128)}, u32[]{:S(2)}) copy-start(f32[4,4,1,1]{1,0,3,2:T(4,128)} %constant.144) | copy-start | bytes 196
  165.1 30.3 %copy-start.14 = (f32[4]{0:T(128)S(1)}, f32[4]{0:T(128)}, u32[]{:S(2)}) copy-start(f32[4]{0:T(128)} %constant.139.clone) | copy-start | bytes 52
  196.1 36.6 %copy-start.8 = (f32[4,4,1,1,1,1]{1,0,5,4,3,2:T(4,128)S(1)}, f32[4,4,1,1,1,1]{1,0,5,4,3,2:T(4,128)}, u32[]{:S(2)}) copy-start(f32[4,4,1,1,1,1]{1,0,5,4,3,2:T(4,128)} %constant.153) | copy-start | bytes 196
Sparse Core Ops, SparseCore 0:
  27.1 74.0 all-gather.2
where the time goes:
time: 252 us; the launch traced here: 251 us
  blocking collectives  96.8 us (38%)
  waiting for transfers between devices  68.7 us (27%)
  matrix products  40.8 us (16%)
  local copies, waits for them, and re-layouts  22.3 us (9%)
  between operations  18.2 us (7%)
  other arithmetic  4.6 us (2%)
    all_gather x1, waiting for transfers between devices, split_hierarchize(): all_firsts = lax.all_gather(first_row[None], 'dom', axis=0, tiled=True)  68.7 us
    dot_general x14, matrix products, apply_table(): jnp.einsum(formula, grid_data, jnp.asarray(matrix, dtype=jnp.float32), pr...  40.8 us
    all_to_all x1, blocking collectives, from_everyone(): return lax.all_to_all(copies, axis, split_axis=0, concat_axis=0, tiled=True)  36.6 us
    all_to_all x1, blocking collectives, sent_and_summed(): lax.all_to_all(parts, axis, split_axis=0, concat_axis=0, tiled=True)  32.1 us
    all_gather x1, blocking collectives, split_dehierarchize(): all_firsts = lax.all_gather(first_row[None], 'dom', axis=0, tiled=True)  28.1 us
    scatter x1, local copies, waits for them, and re-layouts, split_hierarchize(): return result.at[0].set(new_first)  13.8 us
  transfers between devices with their start and end apart: 1, of which 1 were waited for; matrix products, arithmetic and copies ran while one was open for 0% of the time, Pallas kernels for 0%

commit v1 on v0

--- a/solution.py
+++ b/solution.py
@@ -148,7 +148,9 @@
     members = lax.axis_size("dom")
     own_index = lax.axis_index("dom")
     first_row = grid_data[0]
-    all_firsts = lax.all_gather(first_row[None], "dom", axis=0, tiled=True)
+    value = first_row[None]
+    sent = jnp.stack([value] * lax.axis_size("dom"))
+    all_firsts = jnp.concatenate(lax.all_to_all(sent, "dom", 0, 0), axis=0)
     coarse = apply_table(all_firsts, nodal_table(hier_table(members)), 0)
     new_first = lax.dynamic_index_in_dim(coarse, own_index, 0, keepdims=False)
     following = lax.dynamic_index_in_dim(all_firsts, (own_index + 1) % members, 0, keepdims=False)

time: 252 us -> 234 us (0.929)
  waiting for transfers between devices: 68.7 us -> 53.5 us
  between operations: 18.2 us -> 4.77 us
  starting transfers between devices: 0.01 us -> 8.28 us
    all_gather x1 -> x0, waiting for transfers between devices: 68.7 us -> none  [split_hierarchize(): all_firsts = lax.all_gather(first_row[None], 'dom', axis=0, tiled=True)]
    all_to_all x0 -> x1, waiting for transfers between devices: none -> 53.5 us  [split_hierarchize(): all_firsts = jnp.concatenate(lax.all_to_all(sent, 'dom', 0, 0), axis=0)]
    all_to_all x0 -> x1, starting transfers between devices: none -> 8.28 us  [split_hierarchize(): all_firsts = jnp.concatenate(lax.all_to_all(sent, 'dom', 0, 0), axis=0)]
where the time goes in v1:
time: 234 us; the launch traced here: 233 us
  blocking collectives  97.7 us (42%)
  waiting for transfers between devices  53.5 us (23%)
  matrix products  40.6 us (17%)
  local copies, waits for them, and re-layouts  24 us (10%)
  starting transfers between devices  8.28 us (4%)
  between operations  4.77 us (2%)
  other arithmetic  4.6 us (2%)
    all_to_all x1, waiting for transfers between devices, split_hierarchize(): all_firsts = jnp.concatenate(lax.all_to_all(sent, 'dom', 0, 0), axis=0)  53.5 us
    dot_general x14, matrix products, apply_table(): jnp.einsum(formula, grid_data, jnp.asarray(matrix, dtype=jnp.float32), pr...  40.6 us
    all_to_all x1, blocking collectives, from_everyone(): return lax.all_to_all(copies, axis, split_axis=0, concat_axis=0, tiled=True)  36.6 us
    all_to_all x1, blocking collectives, sent_and_summed(): lax.all_to_all(parts, axis, split_axis=0, concat_axis=0, tiled=True)  32.9 us
    all_gather x1, blocking collectives, split_dehierarchize(): all_firsts = lax.all_gather(first_row[None], 'dom', axis=0, tiled=True)  28.2 us
    scatter x1, local copies, waits for them, and re-layouts, split_hierarchize(): return result.at[0].set(new_first)  13.8 us
    all_to_all x1, starting transfers between devices, split_hierarchize(): all_firsts = jnp.concatenate(lax.all_to_all(sent, 'dom', 0, 0), axis=0)  8.28 us
  transfers between devices with their start and end apart: 1, of which 1 were waited for; matrix products, arithmetic and copies ran while one was open for 0% of the time, Pallas kernels for 0%

profile of v1, /device:TPU:1, one launch (start us, length us, event | category | flops | bytes accessed | tf_op | source)
XLA Modules:
  0.0 233.4 jit_solution(14319497212062075188)
XLA Ops:
  0.0 1.6 copy-done
  1.6 5.0 %fusion.21 = f32[4,4,4,8,8,128]{5,1,4,3,2,0:T(4,128)S(1)} fusion(f32[4,4,1,1,1,1]{1,0,5,4,3,2:T(4,128)} %constant.148, f32[4,4,4,8,8,128]{5,4,3,2,1,0:T(8,128)S(1)} %bitcast.101), kind=kOutput, calls=%fused_computation.25 | convolution fusion | flops 25165824 | bytes 4194368 | tf_op jit(solution)/shard_map/abcdef,zb->azcdef/dot_general | solution.py:120
  6.6 4.5 %fusion.24 = f32[4,4,4,8,8,128]{5,2,4,3,1,0:T(4,128)S(1)} fusion(f32[4,4,1,1,1,1]{1,0,5,4,3,2:T(4,128)S(1)} %copy-done.9, f32[4,4,4,8,8,128]{5,1,4,3,2,0:T(4,128)S(1)} %fusion.21), kind=kOutput, calls=%fused_computation.26 | convolution fusion | flops 25165824 | bytes 4194368 | tf_op jit(solution)/shard_map/abcdef,zc->abzdef/dot_general | solution.py:120
  11.2 3.0 %fusion.27 = f32[4,4,4,8,8,128]{5,3,4,2,1,0:T(8,128)S(1)} fusion(f32[8,8,1,1,1,1]{1,0,5,4,3,2:T(8,128)S(1)} %copy-done.7, f32[4,4,4,8,8,128]{5,2,4,3,1,0:T(4,128)S(1)} %fusion.24), kind=kOutput, calls=%fused_computation.27 | convolution fusion | flops 50331648 | bytes 4194560 | tf_op jit(solution)/shard_map/abcdef,zd->abczef/dot_general | solution.py:120
  14.2 2.1 fusion.13
  16.3 1.9 fusion.7
  18.3 1.3 copy-done.1
  19.6 2.5 %stack.3 = f32[8,1,4,4,8,8,128]{6,5,4,3,2,1,0:T(8,128)} broadcast(f32[4,4,8,8,128]{4,3,2,1,0:T(8,128)S(1)} %slice_bitcast_fusion), dimensions={2,3,4,5,6} | broadcast | bytes 4718592 | tf_op jit(solution)/shard_map/stack | solution.py:152
  22.1 8.3 %all-to-all-start = ((f32[8,1,4,4,8,8,128]{6,5,4,3,2,1,0:T(8,128)}), f32[8,1,4,4,8,8,128]{6,5,4,3,2,1,0:T(8,128)}, u32[]{:S(2)}, u32[]{:S(2)}) async-start(f32[8,1,4,4,8,8,128]{6,5,4,3,2,1,0:T(8,128)} %stack.3), calls=%async_computation | async-start | bytes 8388608 | tf_op jit(solution)/shard_map/all_to_all | solution.py:153
  31.1 0.7 fusion.40
  35.9 53.5 %all-to-all-done = f32[8,1,4,4,8,8,128]{6,5,4,3,2,1,0:T(8,128)} async-done(((f32[8,1,4,4,8,8,128]{6,5,4,3,2,1,0:T(8,128)}), f32[8,1,4,4,8,8,128]{6,5,4,3,2,1,0:T(8,128)}, u32[]{:S(2)}, u32[]{:S(2)}) %all-to-all-start) | async-done | bytes 4194336 | tf_op jit(solution)/shard_map/all_to_all | solution.py:153
  89.4 8.1 %fusion = f32[4,4,8,8,128,8]{4,5,3,2,1,0:T(8,128)S(1)} fusion(f32[8,8,1,1,1,1]{1,0,5,4,3,2:T(8,128)S(1)} %copy-done.11, f32[8,1,4,4,8,8,128]{6,5,4,3,2,1,0:T(8,128)} %all-to-all-done), kind=kOutput, calls=%fused_computation | convolution fusion | flops 100663296 | bytes 8388864 | tf_op jit(solution)/shard_map/abcdef,za->zbcdef/dot_general | solution.py:120
  97.6 0.6 dynamic-slice_bitcast_fusion
  98.1 1.1 dynamic-slice_bitcast_fusion.1
  99.3 5.4 %multiply_add_fusion = f32[4,4,4,8,8,128]{5,0,4,3,2,1:T(4,128)} fusion(f32[4,4,1,1,1,1]{1,0,5,4,3,2:T(4,128)S(1)} %copy-done.13, f32[4,4,4,8,8,128]{5,4,3,2,1,0:T(8,128)S(1)} %copy-done.2, f32[4,4,8,8,128]{4,3,2,1,0:T(8,128)S(1)} %dynamic-slice_bitcast_fusion.1, f32[4]{0:T(128)S(1)} %copy-done.15), kind=kOutput, calls=%fused_computation.24 | convolution fusion | flops 26214400 | bytes 4718672 | tf_op jit(solution)/shard_map/abcdef,za->zbcdef/dot_general | solution.py:120
  104.8 13.8 %scatter.6 = f32[4,4,4,8,8,128]{5,0,4,3,2,1:T(4,128)} dynamic-update-slice(f32[4,4,4,8,8,128]{5,0,4,3,2,1:T(4,128)} %multiply_add_fusion, f32[1,4,4,8,8,128]{5,0,4,3,2,1:T(1,128)S(1)} %dynamic-slice_bitcast_fusion, s32[]{:T(128)} %constant.124.clone.1, s32[]{:T(128)} %constant.124.clone.1, s32[]{:T(128)} %constant.124.clone.1, s32[]{:T(128)} %constant.124.clone.1, s32[]{:T(128)} %constant.124.clone.1, ...) | dynamic-update-slice | bytes 1048580 | tf_op jit(solution)/shard_map/scatter | solution.py:163
  118.6 2.3 fusion.3
  120.9 32.9 %all_to_all.15 = f32[16,4,1,8,8,128]{5,1,4,3,2,0:T(4,128)S(1)} all-to-all(f32[16,4,1,8,8,128]{5,1,4,3,2,0:T(4,128)S(1)} %bitcast.102), channel_id=1, replica_groups=mesh['grid'=16,'dom'=8] {'grid'}, dimensions={0} | all-to-all | bytes 4194304 | tf_op jit(solution)/shard_map/all_to_all | solution.py:17
  153.8 0.3 bitcast_reduce_fusion
  154.1 0.3 copy-done.6
  154.4 0.3 convolution_bitcast_fusion.1
  154.8 0.3 convolution_bitcast_fusion
  155.0 0.3 fusion.41
  155.3 28.2 %all-gather = f32[8,8,8,128]{3,2,1,0:T(8,128)S(1)} all-gather(f32[1,8,8,128]{3,2,1,0:T(8,128)S(1)} %slice.118), channel_id=2, replica_groups=mesh['grid'=16,'dom'=8] {'dom'}, dimensions={0}, use_global_device_ids=true | all-gather | bytes 294912 | tf_op jit(solution)/shard_map/all_gather | solution.py:170
  183.5 0.5 fusion.35
  184.1 0.4 convolution_add_fusion
  184.6 0.2 broadcast_in_dim.4
  184.8 36.6 %all_to_all.16 = f32[16,4,1,8,8,128]{5,4,3,1,2,0:T(8,128)S(1)} all-to-all(f32[16,4,1,8,8,128]{5,4,3,1,2,0:T(8,128)S(1)} %broadcast_in_dim.4), channel_id=1, replica_groups=mesh['grid'=16,'dom'=8] {'grid'}, dimensions={0} | all-to-all | bytes 4194304 | tf_op jit(solution)/shard_map/all_to_all | solution.py:29
  221.5 4.3 %fusion.32 = f32[4,4,4,8,8,128]{5,1,4,3,2,0:T(4,128)S(1)} fusion(f32[4,4,1,1,1,1]{1,0,5,4,3,2:T(4,128)S(1)} %copy-done.8, f32[4,4,4,8,8,128]{5,4,3,0,2,1:T(8,128)S(1)} %bitcast.103), kind=kOutput, calls=%fused_computation.28 | convolution fusion | flops 25165824 | bytes 4194368 | tf_op jit(solution)/shard_map/abcdef,zb->azcdef/dot_general | solution.py:120
  225.8 4.3 %fusion.9 = f32[4,4,8,8,128,4]{4,5,3,2,1,0:T(4,128)S(1)} fusion(f32[4,4,1,1,1,1]{1,0,5,4,3,2:T(4,128)S(1)} %copy-done.8, f32[4,4,4,8,8,128]{5,1,4,3,2,0:T(4,128)S(1)} %fusion.32), kind=kOutput, calls=%fused_computation.12 | convolution fusion | flops 25165824 | bytes 4194368 | tf_op jit(solution)/shard_map/abcdef,zc->abzdef/dot_general | solution.py:120
  230.1 1.6 fusion.4
  231.8 1.6 copy.88
  (39 shorter events, 0.5 us)
Async XLA Ops:
  0.0 1.6 copy-start
  1.6 5.0 %copy-start.9 = (f32[4,4,1,1,1,1]{1,0,5,4,3,2:T(4,128)S(1)}, f32[4,4,1,1,1,1]{1,0,5,4,3,2:T(4,128)}, u32[]{:S(2)}) copy-start(f32[4,4,1,1,1,1]{1,0,5,4,3,2:T(4,128)} %constant.148) | copy-start | bytes 196
  6.6 4.5 %copy-start.7 = (f32[8,8,1,1,1,1]{1,0,5,4,3,2:T(8,128)S(1)}, f32[8,8,1,1,1,1]{1,0,5,4,3,2:T(8,128)}, u32[]{:S(2)}) copy-start(f32[8,8,1,1,1,1]{1,0,5,4,3,2:T(8,128)} %constant.149) | copy-start | bytes 772
  14.2 2.1 copy-start.3
  18.3 1.3 copy-start.1
  22.1 8.9 %copy-start.5 = (s32[1,6]{1,0:T(1,128)S(1)}, s32[1,6]{1,0:T(1,128)}, u32[]{:S(2)}) copy-start(s32[1,6]{1,0:T(1,128)} %param.24) | copy-start | bytes 76
  22.1 67.3 %copy-start.11 = (f32[8,8,1,1,1,1]{1,0,5,4,3,2:T(8,128)S(1)}, f32[8,8,1,1,1,1]{1,0,5,4,3,2:T(8,128)}, u32[]{:S(2)}) copy-start(f32[8,8,1,1,1,1]{1,0,5,4,3,2:T(8,128)} %constant.151) | copy-start | bytes 772
  22.1 67.3 %all-to-all-start = ((f32[8,1,4,4,8,8,128]{6,5,4,3,2,1,0:T(8,128)}), f32[8,1,4,4,8,8,128]{6,5,4,3,2,1,0:T(8,128)}, u32[]{:S(2)}, u32[]{:S(2)}) async-start(f32[8,1,4,4,8,8,128]{6,5,4,3,2,1,0:T(8,128)} %stack.3), calls=%async_computation | async-start | bytes 8388608 | tf_op jit(solution)/shard_map/all_to_all | solution.py:153
  89.4 9.9 %copy-start.13 = (f32[4,4,1,1,1,1]{1,0,5,4,3,2:T(4,128)S(1)}, f32[4,4,1,1,1,1]{1,0,5,4,3,2:T(4,128)}, u32[]{:S(2)}) copy-start(f32[4,4,1,1,1,1]{1,0,5,4,3,2:T(4,128)} %constant.147) | copy-start | bytes 196
  97.5 1.7 copy-start.2
  97.6 1.7 copy-start.15
  153.8 0.7 copy-start.6
  153.8 1.3 copy-start.4
  153.8 29.7 %copy-start.10 = (f32[8,8,1,1]{1,0,3,2:T(8,128)S(1)}, f32[8,8,1,1]{1,0,3,2:T(8,128)}, u32[]{:S(2)}) copy-start(f32[8,8,1,1]{1,0,3,2:T(8,128)} %constant.153) | copy-start | bytes 772
  153.8 30.3 %copy-start.12 = (f32[4,4,1,1]{1,0,3,2:T(4,128)S(1)}, f32[4,4,1,1]{1,0,3,2:T(4,128)}, u32[]{:S(2)}) copy-start(f32[4,4,1,1]{1,0,3,2:T(4,128)} %constant.145) | copy-start | bytes 196
  153.8 30.3 %copy-start.14 = (f32[4]{0:T(128)S(1)}, f32[4]{0:T(128)}, u32[]{:S(2)}) copy-start(f32[4]{0:T(128)} %constant.140.clone) | copy-start | bytes 52
  184.8 36.6 %copy-start.8 = (f32[4,4,1,1,1,1]{1,0,5,4,3,2:T(4,128)S(1)}, f32[4,4,1,1,1,1]{1,0,5,4,3,2:T(4,128)}, u32[]{:S(2)}) copy-start(f32[4,4,1,1,1,1]{1,0,5,4,3,2:T(4,128)} %constant.154) | copy-start | bytes 196
